TPU v7x, 32 devices: a 4x4x1 block of a 4x4x8 slice. The times are simulated.
32 devices in a mesh: dp: 1 (over z), cy: 4 (over y), cx: 8 (over x, core).
Axes of the slice: x: 4, y: 4, z: 1, core: 2. Of those that a mesh axis runs over, the one named last changes fastest.
The devices are a block of a 4x4x8 slice.
Arguments:
- q: bfloat16 [4096, 32, 128], P(('dp', 'cy', 'cx'))
- k: bfloat16 [4096, 8, 128], P(('dp', 'cy', 'cx'))
- v: bfloat16 [4096, 8, 128], P(('dp', 'cy', 'cx'))
Outputs:
- output: bfloat16 [4096, 32, 128], P(('dp', 'cy', 'cx'))
All inputs are finite; a program needn't handle non-finite values.
Results may differ from a plain program's by a relative error of at most 0.00348894.
Values are sent between devices in bfloat16 or wider.
A program may use at most 768 MiB of HBM per device.

v0:
```python
import functools
import math

import jax
import jax.numpy as jnp
from jax import lax
from jax.experimental import pallas as pl
from jax.experimental.pallas import tpu as pltpu
from jax.sharding import PartitionSpec as P

NEG = -1.0e30
MESH = pl.DeviceIdType.MESH
F32 = jnp.float32


def kernel(n, c2, q_hbm, kv_hbm, out_hbm, kvbuf, qbuf, vt, acc, mref, lref, ostage,
           ks, kr, qs, qr, gs, gr, os, orx):
    ng, rep, t2, hd = q_hbm.shape
    c = t2 // 2
    nb2 = 2 * n
    half = n * t2
    cols = rep * t2
    dp = lax.axis_index('dp')
    y = lax.axis_index('cy')
    cx = lax.axis_index('cx')
    x = cx // 2
    core = cx % 2
    row_core = core == 0
    own = jnp.where(row_core, y, x)
    pos = jnp.where(row_core, x, y)
    g_me = jnp.where(row_core, x, n + y)

    barrier = pltpu.get_barrier_semaphore()
    cnt = 0
    for d in range(1, 2 * n):
        pl.semaphore_signal(barrier, inc=1, device_id=(dp, y, (cx + d) % (2 * n)), device_id_type=MESH)
        cnt += 1
    for d in range(1, n):
        for cc in range(2):
            pl.semaphore_signal(barrier, inc=1, device_id=(dp, (y + d) % n, 2 * x + cc), device_id_type=MESH)
            cnt += 1
    pl.semaphore_wait(barrier, cnt)

    order = (2, 1, 3, 0) if n == 4 else tuple(range(n))[::-1]

    def spread(fn, sends, recv):
        waits = []
        i = 0
        for d in order:
            for lay in range(2):
                u = x if lay == 0 else y
                j = (u + d) % n
                g = j + lay * n
                dev = (dp, y, 2 * j) if lay == 0 else (dp, j, 2 * x + 1)
                grp = y if lay == 0 else x
                for h in range(2):
                    src, dst = fn(g, grp, u, h)
                    cp = pltpu.make_async_remote_copy(src_ref=src, dst_ref=dst, send_sem=sends.at[i], recv_sem=recv.at[0],
                                                      device_id=dev, device_id_type=MESH)
                    if d == 0:
                        lc = pltpu.make_async_copy(src, dst, recv.at[0])
                        pl.when(core == lay)(lc.start)
                        pl.when(core != lay)(cp.start)
                        waits.append(lambda cp=cp, lay=lay: pl.when(core != lay)(cp.wait_send))
                    else:
                        cp.start()
                        waits.append(cp.wait_send)
                    i += 1
        return waits

    def kv_piece(g, grp, u, h):
        blk = u if h == 0 else nb2 - 1 - u
        sub = core if h == 0 else 1 - core
        off = pl.multiple_of(blk * t2 + sub * c, c)
        return kv_hbm.at[g, :, pl.ds(h * c, c)], kvbuf.at[grp, :, pl.ds(off, c)]

    def q_piece(g, grp, u, h):
        blk = u if h == 0 else nb2 - 1 - u
        sub = core if h == 0 else 1 - core
        off = pl.multiple_of(sub * c, c)
        return q_hbm.at[g, :, pl.ds(h * c, c)], qbuf.at[blk, :, pl.ds(off, c)]

    waits = spread(kv_piece, ks, kr)
    waits += spread(q_piece, qs, qr)

    def me_wait(ref, sem):
        pltpu.make_async_copy(ref, ref, sem).wait()

    def peer(p):
        return (dp, jnp.where(row_core, p, y), jnp.where(row_core, 2 * x, 2 * p + 1))

    me_wait(kvbuf.at[own], kr.at[0])
    for i, d in enumerate((1, 3, 2) if n == 4 else range(1, n)):
        p = (own + d) % n
        for h in range(2):
            part = kvbuf.at[own, :, pl.ds(h * half, half)]
            cp = pltpu.make_async_remote_copy(src_ref=part, dst_ref=part, send_sem=gs.at[2 * i + h],
                                              recv_sem=gr.at[2 * own + h], device_id=peer(p), device_id_type=MESH)
            if h == 0:
                cp.start()
                waits.append(cp.wait_send)
            else:
                need = jnp.logical_or(core == 1, own > p)
                pl.when(need)(cp.start)
                waits.append(lambda cp=cp, need=need: pl.when(need)(cp.wait_send))

    def turn_v(t, base):
        vt[:, pl.ds(base, half)] = kvbuf[t, 1, pl.ds(base, half), :].T

    def attend(a, t, base, nk, diag, first):
        k = kvbuf[t, 0, pl.ds(base, nk), :]
        v = vt[:, pl.ds(base, nk)]
        q = qbuf[a].reshape(cols, hd)
        s = lax.dot_general(k, q, (((1,), (1,)), ((), ())), preferred_element_type=F32)
        if diag:
            key = lax.broadcasted_iota(jnp.int32, (t2, cols), 0)
            row = lax.broadcasted_iota(jnp.int32, (t2, cols), 1) % t2
            last = jnp.where(key <= row, s[nk - t2:], NEG)
            s = last if nk == t2 else jnp.concatenate([s[:nk - t2], last], axis=0)
        mx = jnp.max(s, axis=0, keepdims=True)
        if not first:
            mp = mref[a]
            mx = jnp.maximum(mp, mx)
            alpha = jnp.exp2((mp - mx) * c2)
        mref[a] = mx
        p = jnp.exp2((s - mx) * c2)
        ls = jnp.sum(p, axis=0, keepdims=True)
        pv = lax.dot_general(v, p.astype(jnp.bfloat16), (((1,), (0,)), ((), ())), preferred_element_type=F32)
        if first:
            lref[a] = ls
            acc[a] = pv
        else:
            lref[a] = alpha * lref[a] + ls
            acc[a] = alpha * acc[a] + pv

    me_wait(qbuf, qr.at[0])
    turn_v(own, 0)
    turn_v(own, half)
    for a in range(nb2):
        if a >= n:
            attend(a, own, 0, half, False, True)
            attend(a, own, half, (a - n + 1) * t2, True, False)
        else:
            attend(a, own, 0, (a + 1) * t2, True, True)

    def finish(a):
        o = acc[a] * (1.0 / lref[a])
        for r in range(rep):
            ostage[a, r] = o[:, r * t2:(r + 1) * t2].T.astype(jnp.bfloat16)

    def o_copies(a, h):
        first_half = a < n
        u = jnp.where(first_half, a, nb2 - 1 - a)
        cc = jnp.where(first_half, h, 1 - h)
        dev = (dp, jnp.where(row_core, y, u), jnp.where(row_core, 2 * u, 2 * x) + cc)
        off = pl.multiple_of(jnp.where(first_half, 0, c), c)
        src = ostage.at[a, :, pl.ds(h * c, c)]
        dst = out_hbm.at[g_me, :, pl.ds(off, c)]
        mine = jnp.logical_and(u == pos, cc == core)
        rc = pltpu.make_async_remote_copy(src_ref=src, dst_ref=dst, send_sem=os.at[2 * a + h], recv_sem=orx.at[0],
                                          device_id=dev, device_id_type=MESH)
        return mine, pltpu.make_async_copy(src, dst, orx.at[0]), rc

    def group(i, carry):
        f = jnp.where(i == 0, n - 1, jnp.where(i == 1, 1, 2)) if n == 4 else i + 1
        t = (own + f) % n
        need = jnp.logical_or(core == 1, t > own)
        me_wait(kvbuf.at[t, :, pl.ds(0, half)], gr.at[2 * t])
        turn_v(t, 0)

        @pl.when(need)
        def _():
            me_wait(kvbuf.at[t, :, pl.ds(half, half)], gr.at[2 * t + 1])
            turn_v(t, half)

        def block(ii, carry):
            a = nb2 - 1 - ii
            hi = a >= n
            am = a % n

            @pl.when(hi)
            def _():
                attend(a, t, 0, half, False, False)
            before = jnp.where(hi, t > own, t < own).astype(jnp.int32)
            cntb = jnp.where(row_core, n * before, am + before)
            base = pl.multiple_of(jnp.where(hi, half, 0), half)
            for nb in range(1, n + 1):
                @pl.when(cntb == nb)
                def _(nb=nb):
                    attend(a, t, base, nb * t2, False, False)

            @pl.when(i == n - 2)
            def _():
                finish(a)
                for h in range(2):
                    mine, lc, rc = o_copies(a, h)
                    pl.when(mine)(lc.start)
                    pl.when(jnp.logical_not(mine))(rc.start)
            return carry

        return lax.fori_loop(0, nb2, block, carry)

    lax.fori_loop(0, n - 1, group, 0)

    for w in waits:
        w()

    def drain(a, carry):
        for h in range(2):
            mine, _, rc = o_copies(a, h)
            pl.when(jnp.logical_not(mine))(rc.wait_send)
        return carry

    lax.fori_loop(0, nb2, drain, 0)
    me_wait(out_hbm, orx.at[0])


def solution(mesh):
    n = mesh.shape['cy']
    assert mesh.shape['cx'] == 2 * n
    spec = P(('dp', 'cy', 'cx'))

    def local(q, k, v):
        t, nh, hd = q.shape
        ng = k.shape[1]
        assert ng == 2 * n
        rep = nh // ng
        c2 = hd ** -0.5 * math.log2(math.e)
        qh = q.transpose(1, 0, 2).reshape(ng, rep, t, hd)
        kv = jnp.stack([k.transpose(1, 0, 2), v.transpose(1, 0, 2)], axis=1)
        dma = pltpu.SemaphoreType.DMA
        o = pl.pallas_call(
            functools.partial(kernel, n, c2),
            out_shape=jax.ShapeDtypeStruct((ng, rep, t, hd), q.dtype),
            in_specs=[pl.BlockSpec(memory_space=pl.ANY)] * 2,
            out_specs=pl.BlockSpec(memory_space=pl.ANY),
            scratch_shapes=[
                pltpu.VMEM((n, 2, 2 * n * t, hd), k.dtype),
                pltpu.VMEM((2 * n, rep, t, hd), q.dtype),
                pltpu.VMEM((hd, 2 * n * t), v.dtype),
                pltpu.VMEM((2 * n, hd, rep * t), F32),
                pltpu.VMEM((2 * n, 1, rep * t), F32),
                pltpu.VMEM((2 * n, 1, rep * t), F32),
                pltpu.VMEM((2 * n, rep, t, hd), q.dtype),
                dma((4 * n,)), dma((1,)), dma((4 * n,)), dma((1,)),
                dma((2 * n - 2,)), dma((2 * n,)), dma((4 * n,)), dma((1,)),
            ],
            compiler_params=pltpu.CompilerParams(collective_id=0, has_side_effects=True,
                                                 vmem_limit_bytes=56 * 1024 * 1024),
        )(qh, kv)
        return o.reshape(nh, t, hd).transpose(1, 0, 2)

    return jax.shard_map(local, mesh=mesh, in_specs=(spec, spec, spec), out_specs=spec, check_vma=False)
```

profile of v0, /device:TPU:97, one launch (start us, length us, event | category | flops | bytes accessed | tf_op | source)
XLA Modules:
  0.0 61.2 jit_solution(8342989529828449263)
XLA Ops:
  0.0 0.0 copy-start
  0.0 1.2 %copy_bitcast_fusion.1 = (bf16[8,1,128,128]{3,2,1,0:T(8,128)(2,1)S(1)}, bf16[8,1,128,128]{3,2,1,0:T(8,128)(2,1)S(1)}) fusion(bf16[128,8,128]{2,1,0:T(8,128)(2,1)} %param.5, bf16[128,8,128]{2,1,0:T(8,128)(2,1)} %param.4), kind=kLoop, calls=%fused_computation.2 | loop fusion | bytes 1048576 | tf_op jit(solution)/shard_map/stack | solution.py:230
  1.2 0.9 %pad_maximum_fusion.kv_hbm = bf16[8,2,128,128]{3,2,1,0:T(8,128)(2,1)} fusion(bf16[8,1,128,128]{3,2,1,0:T(8,128)(2,1)S(1)} %get-tuple-element.5, bf16[8,1,128,128]{3,2,1,0:T(8,128)(2,1)S(1)} %get-tuple-element.6), kind=kLoop, calls=%fused_computation.1 | loop fusion | flops 262144 | bytes 1048576 | tf_op jit(solution)/shard_map/stack | solution.py:230
  2.1 0.0 copy-done
  2.1 1.4 %copy.4 = bf16[32,128,128]{2,1,0:T(8,128)(2,1)} copy(bf16[32,128,128]{2,0,1:T(8,128)(2,1)S(1)} %bitcast.16) | data formatting | bytes 2097152 | tf_op jit(solution)/shard_map/transpose | solution.py:229
  3.5 54.9 %shard_map.37 = bf16[8,4,128,128]{3,2,1,0:T(8,128)(2,1)} custom-call(bf16[8,4,128,128]{3,2,1,0:T(8,128)(2,1)} %bitcast.15, bf16[8,2,128,128]{3,2,1,0:T(8,128)(2,1)} %pad_maximum_fusion.kv_hbm), custom_call_target="tpu_custom_call" | custom-call | tf_op jit(solution)/shard_map/pallas_call | solution.py:232
  58.3 2.9 %copy.11 = bf16[32,128,128]{2,0,1:T(8,128)(2,1)} copy(bf16[32,128,128]{2,1,0:T(8,128)(2,1)} %bitcast.14) | data formatting | bytes 2097152 | tf_op jit(solution)/shard_map/reshape | solution.py:251
Async XLA Ops:
  0.0 2.1 %copy-start = (bf16[128,32,128]{2,1,0:T(8,128)(2,1)S(1)}, bf16[128,32,128]{2,1,0:T(8,128)(2,1)}, u32[]{:S(2)}) copy-start(bf16[128,32,128]{2,1,0:T(8,128)(2,1)} %param.3) | copy-start | bytes 3145732
where the time goes:
time: 61.3 us; the launch traced here: 61.2 us
  Pallas kernels  54.9 us (90%)
  local copies, waits for them, and re-layouts  5.46 us (9%)
  other arithmetic  0.86 us (1%)
    pallas_call x1, Pallas kernels, local(): pl.pallas_call(functools.partial(kernel, n, c2), out_shape=jax.ShapeDtype...  54.9 us
    reshape x1, local copies, waits for them, and re-layouts, local(): return o.reshape(nh, t, hd).transpose(1, 0, 2)  2.87 us
    transpose x1, local copies, waits for them, and re-layouts, local(): qh = q.transpose(1, 0, 2).reshape(ng, rep, t, hd)  1.38 us

commit v1 on v0

v1 whole, which is shorter than its diff:
```python
import functools
import math

import jax
import jax.numpy as jnp
from jax import lax
from jax.experimental import pallas as pl
from jax.experimental.pallas import tpu as pltpu
from jax.sharding import PartitionSpec as P

NEG = -1.0e30
MESH = pl.DeviceIdType.MESH
F32 = jnp.float32


def kernel(n, c2, q_hbm, k_hbm, v_hbm, out_hbm, kvbuf, qbuf, qt, vt, s0, s1, s2, s3, x0, x1, x2, x3, acc, mref, lref, ostage,
           ks, kr, qs, qr, gs, gr, os, orx):
    t2, ng, rep, hd = q_hbm.shape
    c = t2 // 2
    nb2 = 2 * n
    half = n * t2
    cols = rep * t2
    dp = lax.axis_index('dp')
    y = lax.axis_index('cy')
    cx = lax.axis_index('cx')
    x = cx // 2
    core = cx % 2
    row_core = core == 0
    own = jnp.where(row_core, y, x)
    pos = jnp.where(row_core, x, y)
    g_me = jnp.where(row_core, x, n + y)

    barrier = pltpu.get_barrier_semaphore()
    cnt = 0
    for d in range(1, 2 * n):
        pl.semaphore_signal(barrier, inc=1, device_id=(dp, y, (cx + d) % (2 * n)), device_id_type=MESH)
        cnt += 1
    for d in range(1, n):
        for cc in range(2):
            pl.semaphore_signal(barrier, inc=1, device_id=(dp, (y + d) % n, 2 * x + cc), device_id_type=MESH)
            cnt += 1
    pl.semaphore_wait(barrier, cnt)

    order = (2, 1, 3, 0) if n == 4 else tuple(range(n))[::-1]

    def spread(fn, sends, recv, split, parts):
        waits = []
        i = 0
        for d in order:
            for lay in range(2):
                u = x if lay == 0 else y
                j = (u + d) % n
                g = j + lay * n
                dev = (dp, y, 2 * j) if lay == 0 else (dp, j, 2 * x + 1)
                grp = y if lay == 0 else x
                for h in range(parts):
                    src, dst = fn(g, grp, u, h)
                    rsem = recv.at[u if split else 0]
                    cp = pltpu.make_async_remote_copy(src_ref=src, dst_ref=dst, send_sem=sends.at[i], recv_sem=rsem,
                                                      device_id=dev, device_id_type=MESH)
                    if d == 0:
                        lc = pltpu.make_async_copy(src, dst, rsem)
                        pl.when(core == lay)(lc.start)
                        pl.when(core != lay)(cp.start)
                        waits.append(lambda cp=cp, lay=lay: pl.when(core != lay)(cp.wait_send))
                    else:
                        cp.start()
                        waits.append(cp.wait_send)
                    i += 1
        return waits

    def kv_piece(g, grp, u, hw):
        h, w = hw % 2, hw // 2
        blk = u if h == 0 else nb2 - 1 - u
        sub = core if h == 0 else 1 - core
        off = pl.multiple_of(blk * t2 + sub * c, c)
        return (k_hbm, v_hbm)[w].at[g, pl.ds(h * c, c)], kvbuf.at[grp, w, pl.ds(off, c)]

    def q_piece(g, grp, u, h):
        blk = u if h == 0 else nb2 - 1 - u
        sub = core if h == 0 else 1 - core
        off = pl.multiple_of(sub * c, c)
        return q_hbm.at[pl.ds(h * c, c), g], qbuf.at[blk, pl.ds(off, c)]

    waits = spread(kv_piece, ks, kr, False, 4)
    waits += spread(q_piece, qs, qr, True, 2)

    def me_wait(ref, sem):
        pltpu.make_async_copy(ref, ref, sem).wait()

    def peer(p):
        return (dp, jnp.where(row_core, p, y), jnp.where(row_core, 2 * x, 2 * p + 1))

    def share_copies():
        for i, d in enumerate((1, 3, 2) if n == 4 else range(1, n)):
            p = (own + d) % n
            for h in range(2):
                part = kvbuf.at[own, :, pl.ds(h * half, half)]
                cp = pltpu.make_async_remote_copy(src_ref=part, dst_ref=part, send_sem=gs.at[2 * i + h],
                                                  recv_sem=gr.at[2 * own + h], device_id=peer(p), device_id_type=MESH)
                yield cp, True if h == 0 else jnp.logical_or(core == 1, own > p)

    def share():
        for cp, need in share_copies():
            pl.when(need)(cp.start)

    def turn_v(t, base):
        vt[:, pl.ds(base, half)] = kvbuf[t, 1, pl.ds(base, half), :].T

    s_bufs = (s0, s1, s2, s3)
    x_bufs = (x0, x1, x2, x3)

    def score(step, t, slot):
        q, b0, nb, diag, _ = step
        k = kvbuf[t, 0, pl.ds(b0 * t2, nb * t2), :]
        s = lax.dot_general(k, qt[q], (((1,), (0,)), ((), ())), preferred_element_type=F32)
        if diag:
            key = lax.broadcasted_iota(jnp.int32, (t2, cols), 0)
            row = lax.broadcasted_iota(jnp.int32, (t2, cols), 1) // rep
            tail = jnp.where(key <= row, s[(nb - 1) * t2:], NEG)
            s = tail if nb == 1 else jnp.concatenate([s[:(nb - 1) * t2], tail], axis=0)
        s_bufs[slot][pl.ds(0, nb * t2), :] = s
        x_bufs[slot][...] = jnp.max(s, axis=0, keepdims=True)

    def fold(step, slot):
        q, b0, nb, _, fresh = step
        s = s_bufs[slot][pl.ds(0, nb * t2), :]
        mx = x_bufs[slot][...]
        if not fresh:
            mp = mref[q]
            mx = jnp.maximum(mp, mx)
            alpha = jnp.exp2((mp - mx) * c2)
        mref[q] = mx
        p = jnp.exp2((s - mx) * c2)
        ls = jnp.sum(p, axis=0, keepdims=True)
        v = vt[:, pl.ds(b0 * t2, nb * t2)]
        pv = lax.dot_general(v, p.astype(jnp.bfloat16), (((1,), (0,)), ((), ())), preferred_element_type=F32)
        if fresh:
            lref[q] = ls
            acc[q] = pv
        else:
            lref[q] = alpha * lref[q] + ls
            acc[q] = alpha * acc[q] + pv

    def run(t, counts, own_group):
        plan = []
        for q, cnt in counts:
            b0 = 0
            while b0 < cnt:
                nb = min(4, cnt - b0)
                plan.append((q, b0, nb, own_group and b0 + nb == cnt, own_group and b0 == 0))
                b0 += nb
        for i in range(min(2, len(plan))):
            score(plan[i], t, i % 4)
        for i, step in enumerate(plan):
            if i + 2 < len(plan):
                score(plan[i + 2], t, (i + 2) % 4)
            fold(step, i % 4)

    def near(i):
        return jnp.where(i == 0, 0, jnp.where(i == 1, n - 1, i - 1))

    parts = (tuple(range(n)), tuple(range(n, n + n // 2)), tuple(range(n + n // 2, nb2)))

    def finish(a):
        o = acc[a] * (1.0 / lref[a])
        ostage[a] = o.T.astype(jnp.bfloat16).reshape(t2, rep, hd)

    def o_copies(a, h):
        first_half = a < n
        u = jnp.where(first_half, a, nb2 - 1 - a)
        cc = jnp.where(first_half, h, 1 - h)
        dev = (dp, jnp.where(row_core, y, u), jnp.where(row_core, 2 * u, 2 * x) + cc)
        off = pl.multiple_of(jnp.where(first_half, 0, c), c)
        src = ostage.at[a, pl.ds(h * c, c)]
        dst = out_hbm.at[pl.ds(off, c), g_me]
        mine = jnp.logical_and(u == pos, cc == core)
        rc = pltpu.make_async_remote_copy(src_ref=src, dst_ref=dst, send_sem=os.at[2 * a + h], recv_sem=orx.at[0],
                                          device_id=dev, device_id_type=MESH)
        return mine, pltpu.make_async_copy(src, dst, orx.at[0]), rc

    def send_out(a):
        finish(a)
        for h in range(2):
            mine, lc, rc = o_copies(a, h)
            pl.when(mine)(lc.start)
            pl.when(jnp.logical_not(mine))(rc.start)

    def turn_q(u):
        me_wait(qbuf.at[pl.ds(0, 2)], qr.at[u])
        for blk in (u, nb2 - 1 - u):
            qt[blk] = qbuf[blk].reshape(cols, hd).T

    def other(t, last, core_is, before):
        for part in parts:
            if core_is == 0:
                counts = [(q, (n if before else 0) if q < n else (n if before else nb2)) for q in part]
            else:
                counts = [(q, q + int(before == (q < n))) for q in part]
            run(t, counts, False)

            @pl.when(last)
            def _(part=part):
                lax.fori_loop(part[0], part[-1] + 1, lambda q, c: (send_out(q), c)[1], 0)

    me_wait(kvbuf.at[own], kr.at[0])
    share()
    turn_v(own, 0)
    turn_v(own, half)
    lax.fori_loop(0, n, lambda i, c: (turn_q((pos + near(i)) % n), c)[1], 0)
    run(own, [(q, q + 1) for q in range(nb2)], True)

    def group(i, carry):
        t = (own + near(i)) % n
        last = i == n - 1
        me_wait(kvbuf.at[t, :, pl.ds(0, half)], gr.at[2 * t])
        turn_v(t, 0)

        @pl.when(jnp.logical_or(core == 1, t > own))
        def _():
            me_wait(kvbuf.at[t, :, pl.ds(half, half)], gr.at[2 * t + 1])
            turn_v(t, half)

        for core_is in range(2):
            for before in (True, False):
                @pl.when(jnp.logical_and(core == core_is, (t < own) == before))
                def _(core_is=core_is, before=before):
                    other(t, last, core_is, before)
        return carry

    lax.fori_loop(1, n, group, 0)

    for w in waits:
        w()
    for cp, need in share_copies():
        pl.when(need)(cp.wait_send)

    def drain(a, carry):
        for h in range(2):
            mine, _, rc = o_copies(a, h)
            pl.when(jnp.logical_not(mine))(rc.wait_send)
        return carry

    lax.fori_loop(0, nb2, drain, 0)
    me_wait(out_hbm, orx.at[0])


def solution(mesh):
    n = mesh.shape['cy']
    assert mesh.shape['cx'] == 2 * n
    spec = P(('dp', 'cy', 'cx'))

    def local(q, k, v):
        t, nh, hd = q.shape
        ng = k.shape[1]
        assert ng == 2 * n
        rep = nh // ng
        c2 = hd ** -0.5 * math.log2(math.e)
        qh = q.reshape(t, ng, rep, hd)
        dma = pltpu.SemaphoreType.DMA
        o = pl.pallas_call(
            functools.partial(kernel, n, c2),
            out_shape=jax.ShapeDtypeStruct((t, ng, rep, hd), q.dtype),
            in_specs=[pl.BlockSpec(memory_space=pl.ANY)] * 3,
            out_specs=pl.BlockSpec(memory_space=pl.ANY),
            scratch_shapes=[
                pltpu.VMEM((n, 2, 2 * n * t, hd), k.dtype),
                pltpu.VMEM((2 * n, t, rep, hd), q.dtype),
                pltpu.VMEM((2 * n, hd, rep * t), q.dtype),
                pltpu.VMEM((hd, 2 * n * t), v.dtype),
                *[pltpu.VMEM((4 * t, rep * t), F32)] * 4,
                *[pltpu.VMEM((1, rep * t), F32)] * 4,
                pltpu.VMEM((2 * n, hd, rep * t), F32),
                pltpu.VMEM((2 * n, 1, rep * t), F32),
                pltpu.VMEM((2 * n, 1, rep * t), F32),
                pltpu.VMEM((2 * n, t, rep, hd), q.dtype),
                dma((8 * n,)), dma((1,)), dma((4 * n,)), dma((n,)),
                dma((2 * n - 2,)), dma((2 * n,)), dma((4 * n,)), dma((1,)),
            ],
            compiler_params=pltpu.CompilerParams(collective_id=0, has_side_effects=True,
                                                 vmem_limit_bytes=56 * 1024 * 1024),
        )(qh, k.transpose(1, 0, 2), v.transpose(1, 0, 2))
        return o.reshape(t, nh, hd)

    return jax.shard_map(local, mesh=mesh, in_specs=(spec, spec, spec), out_specs=spec, check_vma=False)
```

time: 61.3 us -> 47.9 us (0.78)
  Pallas kernels: 54.9 us -> 43.6 us
  local copies, waits for them, and re-layouts: 5.46 us -> 4.18 us
  other arithmetic: 0.86 us -> 0 us
    pallas_call x1, Pallas kernels: 54.9 us -> 43.6 us  [local(): pl.pallas_call(functools.partial(kernel, n, c2), out_shape=jax.ShapeDtype...]
    reshape x1 -> x0, local copies, waits for them, and re-layouts: 2.87 us -> none  [local(): return o.reshape(nh, t, hd).transpose(1, 0, 2)]
    unnamed x2 -> x1, local copies, waits for them, and re-layouts: 0.01 us -> 2.26 us
    another operation x1 -> x0, local copies, waits for them, and re-layouts: 1.21 us -> none  [local(): kv = jnp.stack([k.transpose(1, 0, 2), v.transpose(1, 0, 2)], axis=1)]
    another operation x1 -> x0, other arithmetic: 0.86 us -> none  [local(): kv = jnp.stack([k.transpose(1, 0, 2), v.transpose(1, 0, 2)], axis=1)]
where the time goes in v1:
time: 47.9 us; the launch traced here: 47.7 us
  Pallas kernels  43.6 us (91%)
  local copies, waits for them, and re-layouts  4.18 us (9%)
    pallas_call x1, Pallas kernels, local(): pl.pallas_call(functools.partial(kernel, n, c2), out_shape=jax.ShapeDtype...  43.6 us
    unnamed x1, local copies, waits for them, and re-layouts  2.26 us
    transpose x1, local copies, waits for them, and re-layouts, local(): v.transpose(1, 0, 2)  1.92 us

profile of v1, /device:TPU:97, one launch (start us, length us, event | category | flops | bytes accessed | tf_op | source)
XLA Modules:
  0.0 47.7 jit_solution(151136050037836264)
XLA Ops:
  0.0 1.9 %copy_bitcast_fusion = (bf16[8,128,128]{2,1,0:T(8,128)(2,1)}, bf16[8,128,128]{2,1,0:T(8,128)(2,1)}) fusion(bf16[128,8,128]{2,1,0:T(8,128)(2,1)} %param.5, bf16[128,8,128]{2,1,0:T(8,128)(2,1)} %param.4), kind=kLoop, calls=%fused_computation | loop fusion | bytes 1048576 | tf_op jit(solution)/shard_map/transpose | solution.py:282
  1.9 43.6 %shard_map.37 = bf16[128,8,4,128]{3,2,1,0:T(4,128)(2,1)} custom-call(bf16[128,8,4,128]{3,2,1,0:T(4,128)(2,1)} %bitcast.7, bf16[8,128,128]{2,1,0:T(8,128)(2,1)} %get-tuple-element.6.k_hbm, bf16[8,128,128]{2,1,0:T(8,128)(2,1)} %get-tuple-element.5.v_hbm), custom_call_target="tpu_custom_call" | custom-call | tf_op jit(solution)/shard_map/pallas_call | solution.py:261
  45.5 2.3 %copy.9 = bf16[128,32,128]{2,1,0:T(8,128)(2,1)} copy(bf16[128,32,128]{2,1,0:T(8,128)(2,1)} %bitcast.6) | data formatting | bytes 2097152

commit v2 on v1

--- a/solution.py
+++ b/solution.py
@@ -13,7 +13,7 @@
 F32 = jnp.float32
 
 
-def kernel(n, c2, q_hbm, k_hbm, v_hbm, out_hbm, kvbuf, qbuf, qt, vt, s0, s1, s2, s3, x0, x1, x2, x3, acc, mref, lref, ostage,
+def kernel(n, c2, q_hbm, k_hbm, v_hbm, out_hbm, kraw, wide, ksend, ksem, kvbuf, qbuf, qt, vt, s0, s1, s2, s3, x0, x1, x2, x3, acc, mref, lref, ostage,
            ks, kr, qs, qr, gs, gr, os, orx):
     t2, ng, rep, hd = q_hbm.shape
     c = t2 // 2
@@ -39,6 +39,15 @@
         for cc in range(2):
             pl.semaphore_signal(barrier, inc=1, device_id=(dp, (y + d) % n, 2 * x + cc), device_id_type=MESH)
             cnt += 1
+
+    loads = [pltpu.make_async_copy(src, kraw.at[w], ksem.at[w]) for w, src in enumerate((k_hbm, v_hbm))]
+    for cp in loads:
+        cp.start()
+    for w, cp in enumerate(loads):
+        cp.wait()
+        wide[w] = kraw[w].astype(F32).reshape(t2 * ng, hd)
+        for g in range(ng):
+            ksend[w, g] = wide[w, pl.ds(g, t2, stride=ng), :].astype(jnp.bfloat16)
     pl.semaphore_wait(barrier, cnt)
 
     order = (2, 1, 3, 0) if n == 4 else tuple(range(n))[::-1]
@@ -74,7 +83,7 @@
         blk = u if h == 0 else nb2 - 1 - u
         sub = core if h == 0 else 1 - core
         off = pl.multiple_of(blk * t2 + sub * c, c)
-        return (k_hbm, v_hbm)[w].at[g, pl.ds(h * c, c)], kvbuf.at[grp, w, pl.ds(off, c)]
+        return ksend.at[w, g, pl.ds(h * c, c)], kvbuf.at[grp, w, pl.ds(off, c)]
 
     def q_piece(g, grp, u, h):
         blk = u if h == 0 else nb2 - 1 - u
@@ -91,14 +100,27 @@
     def peer(p):
         return (dp, jnp.where(row_core, p, y), jnp.where(row_core, 2 * x, 2 * p + 1))
 
+    def hand_on(t, h, d, sem):
+        p = (own + d) % n
+        part = kvbuf.at[t, :, pl.ds(h * half, half)]
+        cp = pltpu.make_async_remote_copy(src_ref=part, dst_ref=part, send_sem=gs.at[sem], recv_sem=gr.at[2 * t + h],
+                                          device_id=peer(p), device_id_type=MESH)
+        return cp, True if h == 0 else jnp.logical_or(core == 1, t > p)
+
     def share_copies():
-        for i, d in enumerate((1, 3, 2) if n == 4 else range(1, n)):
-            p = (own + d) % n
-            for h in range(2):
-                part = kvbuf.at[own, :, pl.ds(h * half, half)]
-                cp = pltpu.make_async_remote_copy(src_ref=part, dst_ref=part, send_sem=gs.at[2 * i + h],
-                                                  recv_sem=gr.at[2 * own + h], device_id=peer(p), device_id_type=MESH)
-                yield cp, True if h == 0 else jnp.logical_or(core == 1, own > p)
+        return [hand_on(own, h, d, sem) for sem, (h, d) in enumerate(((0, 1), (1, n - 1), (1, 1), (0, n - 1)))]
+
+    prev, after = (own + n - 1) % n, (own + 1) % n
+
+    def relay_copies():
+        return [hand_on(prev, 0, 1, 4), hand_on(after, 1, n - 1, 5)]
+
+    def relay():
+        for (cp, need), t, h in zip(relay_copies(), (prev, after), (0, 1)):
+            @pl.when(need)
+            def _(cp=cp, t=t, h=h):
+                me_wait(kvbuf.at[t, :, pl.ds(h * half, half)], gr.at[2 * t + h])
+                cp.start()
 
     def share():
         for cp, need in share_copies():
@@ -210,15 +232,18 @@
     lax.fori_loop(0, n, lambda i, c: (turn_q((pos + near(i)) % n), c)[1], 0)
     run(own, [(q, q + 1) for q in range(nb2)], True)
 
+    relay()
+
     def group(i, carry):
         t = (own + near(i)) % n
         last = i == n - 1
-        me_wait(kvbuf.at[t, :, pl.ds(0, half)], gr.at[2 * t])
+        pl.when(i != 1)(lambda: me_wait(kvbuf.at[t, :, pl.ds(0, half)], gr.at[2 * t]))
         turn_v(t, 0)
 
         @pl.when(jnp.logical_or(core == 1, t > own))
         def _():
-            me_wait(kvbuf.at[t, :, pl.ds(half, half)], gr.at[2 * t + 1])
+            relayed = jnp.logical_and(i == 2, jnp.logical_or(core == 1, t > prev))
+            pl.when(jnp.logical_not(relayed))(lambda: me_wait(kvbuf.at[t, :, pl.ds(half, half)], gr.at[2 * t + 1]))
             turn_v(t, half)
 
         for core_is in range(2):
@@ -232,7 +257,7 @@
 
     for w in waits:
         w()
-    for cp, need in share_copies():
+    for cp, need in share_copies() + relay_copies():
         pl.when(need)(cp.wait_send)
 
     def drain(a, carry):
@@ -247,7 +272,7 @@
 
 def solution(mesh):
     n = mesh.shape['cy']
-    assert mesh.shape['cx'] == 2 * n
+    assert n == 4 and mesh.shape['cx'] == 2 * n
     spec = P(('dp', 'cy', 'cx'))
 
     def local(q, k, v):
@@ -264,6 +289,10 @@
             in_specs=[pl.BlockSpec(memory_space=pl.ANY)] * 3,
             out_specs=pl.BlockSpec(memory_space=pl.ANY),
             scratch_shapes=[
+                pltpu.VMEM((2, t, ng, hd), k.dtype),
+                pltpu.VMEM((2, t * ng, hd), F32),
+                pltpu.VMEM((2, ng, t, hd), k.dtype),
+                dma((2,)),
                 pltpu.VMEM((n, 2, 2 * n * t, hd), k.dtype),
                 pltpu.VMEM((2 * n, t, rep, hd), q.dtype),
                 pltpu.VMEM((2 * n, hd, rep * t), q.dtype),
@@ -279,7 +308,7 @@
             ],
             compiler_params=pltpu.CompilerParams(collective_id=0, has_side_effects=True,
                                                  vmem_limit_bytes=56 * 1024 * 1024),
-        )(qh, k.transpose(1, 0, 2), v.transpose(1, 0, 2))
+        )(qh, k, v)
         return o.reshape(t, nh, hd)
 
     return jax.shard_map(local, mesh=mesh, in_specs=(spec, spec, spec), out_specs=spec, check_vma=False)

time: 47.9 us -> 41.5 us (0.87)
  Pallas kernels: 43.6 us -> 39.1 us
  local copies, waits for them, and re-layouts: 4.18 us -> 2.26 us
    pallas_call x1, Pallas kernels: 43.6 us -> 39.1 us  [local(): pl.pallas_call(functools.partial(kernel, n, c2), out_shape=jax.ShapeDtype...]
    transpose x1 -> x0, local copies, waits for them, and re-layouts: 1.92 us -> none  [local(): v.transpose(1, 0, 2)]
where the time goes in v2:
time: 41.5 us; the launch traced here: 41.4 us
  Pallas kernels  39.1 us (94%)
  local copies, waits for them, and re-layouts  2.26 us (5%)
    pallas_call x1, Pallas kernels, local(): pl.pallas_call(functools.partial(kernel, n, c2), out_shape=jax.ShapeDtype...  39.1 us
    unnamed x1, local copies, waits for them, and re-layouts  2.26 us

profile of v2, /device:TPU:97, one launch (start us, length us, event | category | flops | bytes accessed | tf_op | source)
XLA Modules:
  0.0 41.4 jit_solution(7943888939101085529)
XLA Ops:
  0.0 39.1 %shard_map.37 = bf16[128,8,4,128]{3,2,1,0:T(4,128)(2,1)} custom-call(bf16[128,8,4,128]{3,2,1,0:T(4,128)(2,1)} %bitcast.3, bf16[128,8,128]{2,1,0:T(8,128)(2,1)} %k_hbm.1, bf16[128,8,128]{2,1,0:T(8,128)(2,1)} %v_hbm.1), custom_call_target="tpu_custom_call" | custom-call | tf_op jit(solution)/shard_map/pallas_call | solution.py:286
  39.1 2.3 %copy.5 = bf16[128,32,128]{2,1,0:T(8,128)(2,1)} copy(bf16[128,32,128]{2,1,0:T(8,128)(2,1)} %bitcast.2) | data formatting | bytes 2097152

commit v3 on v2

--- a/solution.py
+++ b/solution.py
@@ -50,9 +50,8 @@
             ksend[w, g] = wide[w, pl.ds(g, t2, stride=ng), :].astype(jnp.bfloat16)
     pl.semaphore_wait(barrier, cnt)
 
-    order = (2, 1, 3, 0) if n == 4 else tuple(range(n))[::-1]
-
-    def spread(fn, sends, recv, split, parts):
+
+    def spread(fn, sends, recv, split, parts, order):
         waits = []
         i = 0
         for d in order:
@@ -91,8 +90,8 @@
         off = pl.multiple_of(sub * c, c)
         return q_hbm.at[pl.ds(h * c, c), g], qbuf.at[blk, pl.ds(off, c)]
 
-    waits = spread(kv_piece, ks, kr, False, 4)
-    waits += spread(q_piece, qs, qr, True, 2)
+    waits = spread(kv_piece, ks, kr, False, 4, (2, 1, 3, 0))
+    waits += spread(q_piece, qs, qr, True, 2, (0, 1, 3, 2))
 
     def me_wait(ref, sem):
         pltpu.make_async_copy(ref, ref, sem).wait()
@@ -164,14 +163,15 @@
             lref[q] = alpha * lref[q] + ls
             acc[q] = alpha * acc[q] + pv
 
-    def run(t, counts, own_group):
+    def run(t, ranges, own_group):
         plan = []
-        for q, cnt in counts:
-            b0 = 0
-            while b0 < cnt:
-                nb = min(4, cnt - b0)
-                plan.append((q, b0, nb, own_group and b0 + nb == cnt, own_group and b0 == 0))
+        for q, b0, b1 in ranges:
+            fresh = own_group
+            while b0 < b1:
+                nb = min(4, b1 - b0)
+                plan.append((q, b0, nb, own_group and b0 + nb == b1, fresh))
                 b0 += nb
+                fresh = False
         for i in range(min(2, len(plan))):
             score(plan[i], t, i % 4)
         for i, step in enumerate(plan):
@@ -181,8 +181,6 @@
 
     def near(i):
         return jnp.where(i == 0, 0, jnp.where(i == 1, n - 1, i - 1))
-
-    parts = (tuple(range(n)), tuple(range(n, n + n // 2)), tuple(range(n + n // 2, nb2)))
 
     def finish(a):
         o = acc[a] * (1.0 / lref[a])
@@ -213,47 +211,78 @@
         for blk in (u, nb2 - 1 - u):
             qt[blk] = qbuf[blk].reshape(cols, hd).T
 
-    def other(t, last, core_is, before):
-        for part in parts:
-            if core_is == 0:
-                counts = [(q, (n if before else 0) if q < n else (n if before else nb2)) for q in part]
-            else:
-                counts = [(q, q + int(before == (q < n))) for q in part]
-            run(t, counts, False)
-
-            @pl.when(last)
-            def _(part=part):
-                lax.fori_loop(part[0], part[-1] + 1, lambda q, c: (send_out(q), c)[1], 0)
+    def reach(core_is, before, q):
+        if core_is == 0:
+            return (n if before else 0) if q < n else (n if before else nb2)
+        return q + int(before == (q < n))
+
+    def other(t, core_is, before, blocks, halves):
+        ranges = []
+        for q in blocks:
+            for h in halves:
+                ranges.append((q, h * n, min(reach(core_is, before, q), (h + 1) * n)))
+        run(t, ranges, False)
+
+    def each_form(t, fn, also=None):
+        for core_is in range(2):
+            for bf in (True, False):
+                cond = jnp.logical_and(core == core_is, (t < own) == bf)
+                pl.when(cond if also is None else jnp.logical_and(cond, also))(functools.partial(fn, core_is, bf))
+
+    def send_range(lo, hi):
+        lax.fori_loop(lo, hi, lambda q, c: (send_out(q), c)[1], 0)
 
     me_wait(kvbuf.at[own], kr.at[0])
     share()
     turn_v(own, 0)
     turn_v(own, half)
-    lax.fori_loop(0, n, lambda i, c: (turn_q((pos + near(i)) % n), c)[1], 0)
-    run(own, [(q, q + 1) for q in range(nb2)], True)
-
+    def own_pair(i, carry):
+        u = (pos + near(i)) % n
+        turn_q(u)
+        for k in range(n):
+            @pl.when(u == k)
+            def _(k=k):
+                run(own, [(q, 0, q + 1) for q in (nb2 - 1 - k, k)], True)
+        return carry
+
+    lax.fori_loop(0, n, own_pair, 0)
     relay()
 
-    def group(i, carry):
-        t = (own + near(i)) % n
-        last = i == n - 1
-        pl.when(i != 1)(lambda: me_wait(kvbuf.at[t, :, pl.ds(0, half)], gr.at[2 * t]))
-        turn_v(t, 0)
-
-        @pl.when(jnp.logical_or(core == 1, t > own))
+    def take(t, h, in_relay):
+        base = pl.multiple_of(h * half, half)
+
+        @pl.when(jnp.logical_or(h == 0, jnp.logical_or(core == 1, t > own)))
         def _():
-            relayed = jnp.logical_and(i == 2, jnp.logical_or(core == 1, t > prev))
-            pl.when(jnp.logical_not(relayed))(lambda: me_wait(kvbuf.at[t, :, pl.ds(half, half)], gr.at[2 * t + 1]))
-            turn_v(t, half)
-
-        for core_is in range(2):
-            for before in (True, False):
-                @pl.when(jnp.logical_and(core == core_is, (t < own) == before))
-                def _(core_is=core_is, before=before):
-                    other(t, last, core_is, before)
+            @pl.when(jnp.logical_not(in_relay))
+            def _():
+                me_wait(kvbuf.at[t, :, pl.ds(base, half)], gr.at[2 * t + h])
+            turn_v(t, base)
+
+    def phase(i, carry):
+        t = (own + jnp.where(i % 2 == 0, n - 1, 1)) % n
+        h = jnp.where(jnp.logical_or(i == 1, i == 2), 1, 0)
+        take(t, h, jnp.logical_or(i == 0, jnp.logical_and(i == 1, jnp.logical_or(core == 1, after > prev))))
+        for hh in range(2):
+            each_form(t, lambda core_is, bf, hh=hh: other(t, core_is, bf, range(n * hh, nb2) if hh else range(nb2), (hh,)), h == hh)
         return carry
 
-    lax.fori_loop(1, n, group, 0)
+    lax.fori_loop(0, n, phase, 0)
+
+    far = (own + 2) % n
+    take(far, 0, core < 0)
+    each_form(far, lambda core_is, bf: other(far, core_is, bf, range(n), (0,)))
+    send_range(0, n)
+    take(far, 1, core < 0)
+
+    def tail(i, carry):
+        w = jnp.where(pos < n // 2, i, 1 - i)
+        for ww in range(2):
+            lo = n + ww * (n // 2)
+            each_form(far, lambda core_is, bf, lo=lo: other(far, core_is, bf, range(lo, lo + n // 2), (0, 1)), w == ww)
+        send_range(n + w * (n // 2), n + (w + 1) * (n // 2))
+        return carry
+
+    lax.fori_loop(0, 2, tail, 0)
 
     for w in waits:
         w()

time: 41.5 us -> 38.4 us (0.925)
  Pallas kernels: 39.1 us -> 36 us
    pallas_call x1, Pallas kernels: 39.1 us -> 36 us  [local(): pl.pallas_call(functools.partial(kernel, n, c2), out_shape=jax.ShapeDtype...]
where the time goes in v3:
time: 38.4 us; the launch traced here: 38.3 us
  Pallas kernels  36 us (94%)
  local copies, waits for them, and re-layouts  2.26 us (6%)
    pallas_call x1, Pallas kernels, local(): pl.pallas_call(functools.partial(kernel, n, c2), out_shape=jax.ShapeDtype...  36 us
    unnamed x1, local copies, waits for them, and re-layouts  2.26 us

profile of v3, /device:TPU:97, one launch (start us, length us, event | category | flops | bytes accessed | tf_op | source)
XLA Modules:
  0.0 38.3 jit_solution(5508691778237105032)
XLA Ops:
  0.0 36.0 %shard_map.37 = bf16[128,8,4,128]{3,2,1,0:T(4,128)(2,1)} custom-call(bf16[128,8,4,128]{3,2,1,0:T(4,128)(2,1)} %bitcast.3, bf16[128,8,128]{2,1,0:T(8,128)(2,1)} %k_hbm.1, bf16[128,8,128]{2,1,0:T(8,128)(2,1)} %v_hbm.1), custom_call_target="tpu_custom_call" | custom-call | tf_op jit(solution)/shard_map/pallas_call | solution.py:315
  36.0 2.3 %copy.5 = bf16[128,32,128]{2,1,0:T(8,128)(2,1)} copy(bf16[128,32,128]{2,1,0:T(8,128)(2,1)} %bitcast.2) | data formatting | bytes 2097152

commit v4 on v3

--- a/solution.py
+++ b/solution.py
@@ -172,11 +172,11 @@
                 plan.append((q, b0, nb, own_group and b0 + nb == b1, fresh))
                 b0 += nb
                 fresh = False
-        for i in range(min(2, len(plan))):
+        for i in range(min(3, len(plan))):
             score(plan[i], t, i % 4)
         for i, step in enumerate(plan):
-            if i + 2 < len(plan):
-                score(plan[i + 2], t, (i + 2) % 4)
+            if i + 3 < len(plan):
+                score(plan[i + 3], t, (i + 3) % 4)
             fold(step, i % 4)
 
     def near(i):

time: 38.4 us -> 38.3 us (level)
  no operation moved by 1% of the time
where the time goes in v4:
time: 38.3 us; the launch traced here: 38.2 us
  Pallas kernels  35.9 us (94%)
  local copies, waits for them, and re-layouts  2.26 us (6%)
    pallas_call x1, Pallas kernels, local(): pl.pallas_call(functools.partial(kernel, n, c2), out_shape=jax.ShapeDtype...  35.9 us
    unnamed x1, local copies, waits for them, and re-layouts  2.26 us

profile of v4, /device:TPU:97, one launch (start us, length us, event | category | flops | bytes accessed | tf_op | source)
XLA Modules:
  0.0 38.2 jit_solution(2618243604679914800)
XLA Ops:
  0.0 35.9 %shard_map.37 = bf16[128,8,4,128]{3,2,1,0:T(4,128)(2,1)} custom-call(bf16[128,8,4,128]{3,2,1,0:T(4,128)(2,1)} %bitcast.3, bf16[128,8,128]{2,1,0:T(8,128)(2,1)} %k_hbm.1, bf16[128,8,128]{2,1,0:T(8,128)(2,1)} %v_hbm.1), custom_call_target="tpu_custom_call" | custom-call | tf_op jit(solution)/shard_map/pallas_call | solution.py:315
  35.9 2.3 %copy.5 = bf16[128,32,128]{2,1,0:T(8,128)(2,1)} copy(bf16[128,32,128]{2,1,0:T(8,128)(2,1)} %bitcast.2) | data formatting | bytes 2097152
